TPU v7x, 32 devices: a whole 2x2x4 slice. The times are simulated.
32 devices in a mesh: gx: 16 (over z, y, core), gy: 2 (over x).
Axes of the slice: x: 2, y: 2, z: 4, core: 2. Of those that a mesh axis runs over, the one named last changes fastest.
Arguments:
- right_side: float32 [16, 2, 512, 256], P('gx', 'gy'), may hold values from -8 to 8, as said below
- coords: float32 [16, 2, 2, 512], P('gx', 'gy'), may hold values from 0 to 1
- noise: float32 [16, 2, 512], P('gx', 'gy'), may hold values from 0.25 to 1
- intersect: int32 [16, 2, 128], P('gx', 'gy'), may hold values from 0 to 4607, as said below
Outputs:
- solution: float32 [16, 2, 512, 256], P('gx', 'gy')
- residual: float32 [16, 2, 512, 256], P('gx', 'gy')
Inputs may be any that keep to these rules, and one draw needn't show every extreme that they name: `right_side`: right-hand sides of order one. `intersect`: each subdomain's list holds 128 distinct indices in increasing order; none names the subdomain itself (block number 4) or a subdomain beyond the first or last one along the second dimension.
All inputs are finite; a program needn't handle non-finite values.
Results may differ from a plain program's by a relative error of at most 0.0003.
Values sent between devices are 32-bit elements; how exact they have to be, the bound alone decides.
A program may use at most 128 MiB of HBM per device.

v0:
```python
import math
import jax
import jax.numpy as jnp
from jax import lax
from jax.sharding import PartitionSpec as P

ITERS = 3
RANGE_LEN = 0.25
ROOT_THREE = math.sqrt(3.0)
HIGH = lax.Precision.HIGHEST


def shifted(value, axis, by):
    count = lax.axis_size(axis)
    return lax.ppermute(value, axis, [(i, (i + by) % count) for i in range(count)])


def passed_along(block, axis, distance):
    devices = range(lax.axis_size(axis))
    route = [(i - distance, i) for i in devices if i - distance in devices]
    return lax.ppermute(block, axis, route)


def kernel_block(rows_pos, cols_pos):
    delta_x = rows_pos[0][:, None] - cols_pos[0][None, :]
    delta_y = rows_pos[1][:, None] - cols_pos[1][None, :]
    distance = jnp.sqrt(delta_x * delta_x + delta_y * delta_y)
    scaled = ROOT_THREE / RANGE_LEN * distance
    clipped = jnp.minimum(distance, 1.0)
    taper_val = jnp.square(jnp.square(1.0 - clipped)) * (4.0 * clipped + 1.0)
    return (1.0 + scaled) * jnp.exp(-scaled) * taper_val


def window_values(values):
    beside = {}
    for step_by in (1, -1):
        beside[step_by] = shifted(values, "gx", step_by)
    column = jnp.stack([beside[1], values, beside[-1]])
    across = {}
    for step_by in (1, -1):
        across[step_by] = passed_along(column, "gy", step_by)
    return [across[1], column, across[-1]]


def window_index(values):
    beside = {}
    for step_by in (1, -1):
        beside[step_by] = shifted(values, "gx", step_by)
    column = jnp.stack([beside[1], values, beside[-1]])
    across = {}
    for step_by in (1, -1):
        across[step_by] = passed_along(column, "gy", step_by)
    return [across[1], column, across[-1]]


def column_sum(first, second):
    return jnp.sum(first * second, axis=0)


def residual_dot(residue, precond):
    return lax.psum(column_sum(residue, precond), ("gx", "gy"))


def shards(right_side, coords, noise, intersect):
    points = right_side.shape[2]
    rhs_count = right_side.shape[3]
    intersect_len = intersect.shape[2]
    ext_len = points + intersect_len
    own_pos = coords.reshape(2, points)
    own_noise = noise.reshape(points)
    point_info = jnp.concatenate([own_pos, own_noise[None, :]], axis=0)
    info_cols = window_values(point_info)
    positions = [
        [
            jnp.stack(
                [
                    info_cols[col_off][row_off, 0] + float(row_off - 1),
                    info_cols[col_off][row_off, 1] + float(col_off - 1),
                ]
            )
            for col_off in range(3)
        ]
        for row_off in range(3)
    ]
    intersect_ids = intersect.reshape(intersect_len)
    block_id = intersect_ids // points
    row_in = intersect_ids % points
    row_of = block_id // 3
    col_of = block_id % 3
    local_id = row_of * points + row_in
    picked_info = [
        jnp.take(
            jnp.transpose(info_cols[col_off], (1, 0, 2)).reshape(3, 3 * points), local_id, axis=1
        )
        for col_off in range(3)
    ]
    chosen = jnp.where(
        col_of[None, :] == 0,
        picked_info[0],
        jnp.where(col_of[None, :] == 1, picked_info[1], picked_info[2]),
    )
    ov_pos = jnp.stack(
        [chosen[0] + (row_of - 1).astype(jnp.float32), chosen[1] + (col_of - 1).astype(jnp.float32)]
    )
    ext_pos = jnp.concatenate([own_pos, ov_pos], axis=1)
    ext_noise = jnp.concatenate([own_noise, chosen[2]])
    local_matrix = kernel_block(ext_pos, ext_pos) + jnp.diag(ext_noise)
    factor = jnp.linalg.cholesky(local_matrix)
    inv_factor = lax.linalg.triangular_solve(
        factor, jnp.eye(ext_len, dtype=jnp.float32), left_side=True, lower=True
    )
    inverse = jnp.dot(inv_factor.T, inv_factor, precision=HIGH, preferred_element_type=jnp.float32)
    near_ids = window_index(intersect_ids)
    point_iota = jnp.arange(points, dtype=jnp.int32)[:, None]
    row_base = (2 - jnp.arange(3, dtype=jnp.int32))[:, None] * 3
    selectors = []
    for col_off in range(3):
        own_rows = near_ids[col_off] - (row_base + (2 - col_off)) * points
        selectors.append((point_iota == own_rows.reshape(1, 3 * intersect_len)).astype(jnp.float32))

    def borrowed_rows(residue):
        requested = [
            lax.dot_general(
                selectors[col_off],
                residue,
                (((0,), (0,)), ((), ())),
                precision=HIGH,
                preferred_element_type=jnp.float32,
            ).reshape(3, intersect_len, rhs_count)
            for col_off in range(3)
        ]
        combined = jnp.stack([requested[col_off][1] for col_off in range(3)])
        for step_by, row_off in ((-1, 0), (1, 2)):
            outgoing = jnp.stack([requested[col_off][row_off] for col_off in range(3)])
            combined = combined + shifted(outgoing, "gx", step_by)
        gathered = combined[1]
        for step_by, col_off in ((-1, 0), (1, 2)):
            gathered = gathered + passed_along(combined[col_off], "gy", step_by)
        return gathered

    def precondition(residue):
        gathered = borrowed_rows(residue)
        extended = jnp.concatenate([residue, gathered], axis=0)
        solved = jnp.dot(inverse, extended, precision=HIGH, preferred_element_type=jnp.float32)
        returned = window_values(solved[points:])
        result = solved[:points]
        for col_off in range(3):
            result = result + jnp.dot(
                selectors[col_off],
                returned[col_off].reshape(3 * intersect_len, rhs_count),
                precision=HIGH,
                preferred_element_type=jnp.float32,
            )
        return result

    noise_col = own_noise[:, None]
    residual = right_side.reshape(points, rhs_count)
    solution = jnp.zeros_like(residual)
    precond = precondition(residual)
    direction = precond
    inner_now = residual_dot(residual, precond)
    for iteration in range(ITERS):
        columns = window_values(direction)
        accumulated = noise_col * direction
        for operate_row_off in range(3):
            for operate_col_off in range(3):
                accumulated = accumulated + jnp.dot(
                    kernel_block(own_pos, positions[operate_row_off][operate_col_off]),
                    columns[operate_col_off][operate_row_off],
                    precision=HIGH,
                    preferred_element_type=jnp.float32,
                )
        step_size = inner_now / lax.psum(column_sum(direction, accumulated), ("gx", "gy"))
        solution = solution + step_size * direction
        residual = residual - step_size * accumulated
        if iteration + 1 < ITERS:
            precond = precondition(residual)
            inner_next = residual_dot(residual, precond)
            direction = precond + inner_next / inner_now * direction
            inner_now = inner_next
    return (solution.reshape(1, 1, points, rhs_count), residual.reshape(1, 1, points, rhs_count))


def solution(mesh):
    placed = (
        P("gx", "gy", None, None),
        P("gx", "gy", None, None),
        P("gx", "gy", None),
        P("gx", "gy", None),
    )
    return jax.shard_map(
        shards,
        mesh=mesh,
        in_specs=placed,
        out_specs=(P("gx", "gy", None, None), P("gx", "gy", None, None)),
        check_vma=False,
    )
```

profile of v0, /device:TPU:0, one launch (start us, length us, event | category | flops | bytes accessed | tf_op | source)
XLA Modules:
  0.0 750.6 jit_solution(9324209336027450057)
XLA Ops:
  1.2 5.0 collective-permute-start.5
  7.0 4.4 collective-permute-start.1
  15.4 4.5 collective-permute-start.6
  23.5 3.7 collective-permute-start.2
  38.7 11.7 %cholesky.132 = f32[128,128]{1,0:T(8,128)S(1)} custom-call(f32[128,128]{1,0:T(8,128)S(1)} %cholesky.337), custom_call_target="Cholesky" | custom-call | tf_op jit(solution)/shard_map/jit(cholesky)/cholesky | solution.py:108
  50.6 9.8 %custom-call.38 = f32[1,128,128]{1,2,0:T(8,128)S(1)} custom-call(f32[1,128,128]{2,1,0:T(8,128)S(1)} %get-tuple-element.83), custom_call_target="InvertDiagBlocksLowerTriangular" | custom-call | tf_op jit(solution)/shard_map/jit(cholesky)/cholesky | solution.py:108
  63.0 11.9 %cholesky.270 = f32[128,128]{1,0:T(8,128)S(1)} custom-call(f32[128,128]{1,0:T(8,128)S(1)} %cholesky.341), custom_call_target="Cholesky" | custom-call | tf_op jit(solution)/shard_map/jit(cholesky)/cholesky | solution.py:108
  76.3 9.8 %custom-call.39 = f32[1,128,128]{1,2,0:T(8,128)S(1)} custom-call(f32[1,128,128]{2,1,0:T(8,128)S(1)} %get-tuple-element.80), custom_call_target="InvertDiagBlocksLowerTriangular" | custom-call | tf_op jit(solution)/shard_map/jit(cholesky)/cholesky | solution.py:108
  87.8 11.7 %cholesky.291 = f32[128,128]{1,0:T(8,128)S(1)} custom-call(f32[128,128]{1,0:T(8,128)S(1)} %cholesky.346), custom_call_target="Cholesky" | custom-call | tf_op jit(solution)/shard_map/jit(cholesky)/cholesky | solution.py:108
  100.3 9.8 %custom-call.40 = f32[1,128,128]{1,2,0:T(8,128)S(1)} custom-call(f32[1,128,128]{2,1,0:T(8,128)S(1)} %get-tuple-element.77), custom_call_target="InvertDiagBlocksLowerTriangular" | custom-call | tf_op jit(solution)/shard_map/jit(cholesky)/cholesky | solution.py:108
  112.0 11.7 %cholesky.310 = f32[128,128]{1,0:T(8,128)S(1)} custom-call(f32[128,128]{1,0:T(8,128)S(1)} %cholesky.351), custom_call_target="Cholesky" | custom-call | tf_op jit(solution)/shard_map/jit(cholesky)/cholesky | solution.py:108
  124.4 9.8 %custom-call.41 = f32[1,128,128]{1,2,0:T(8,128)S(1)} custom-call(f32[1,128,128]{2,1,0:T(8,128)S(1)} %get-tuple-element.74), custom_call_target="InvertDiagBlocksLowerTriangular" | custom-call | tf_op jit(solution)/shard_map/jit(cholesky)/cholesky | solution.py:108
  135.7 11.7 %cholesky.327 = f32[128,128]{1,0:T(8,128)S(1)} custom-call(f32[128,128]{1,0:T(8,128)S(1)} %convolution_subtract_fusion.6), custom_call_target="Cholesky" | custom-call | tf_op jit(solution)/shard_map/jit(cholesky)/cholesky | solution.py:108
  152.5 17.8 %while.1 = (s32[]{:T(128)}, f32[640,640]{1,0:T(8,128)}, s32[5,2]{0,1:T(2,128)S(1)}, f32[5,128,128]{2,1,0:T(8,128)}, s32[]{:T(128)}) while((s32[]{:T(128)}, f32[640,640]{1,0:T(8,128)}, s32[5,2]{0,1:T(2,128)S(1)}, f32[5,128,128]{2,1,0:T(8,128)}, s32[]{:T(128)}) %tuple.96), condition=%wide.while_cond, body=%wide.while_body.sunk | while | flops 2 | bytes 132705 | solution.py:109
  170.3 50.7 %custom-call.42 = f32[5,128,128]{1,2,0:T(8,128)} custom-call(f32[5,128,128]{2,1,0:T(8,128)} %get-tuple-element.10), custom_call_target="InvertDiagBlocksLowerTriangular" | custom-call | tf_op jit(solution)/shard_map/triangular_solve | solution.py:109
  234.1 4.7 collective-permute-start.11
  238.8 5.0 fusion.240
  245.7 4.4 collective-permute-start.13
  260.4 3.8 collective-permute-done.15
  264.9 4.4 collective-permute-start.17
  269.3 6.9 collective-permute-done.16
  285.3 26.6 %collective-permute-done.18 = f32[3,512,256]{2,1,0:T(8,128)S(1)} collective-permute-done((f32[3,512,256]{2,1,0:T(8,128)S(1)}, f32[3,512,256]{2,1,0:T(8,128)S(1)}, u32[]{:S(2)}, u32[]{:S(2)}) %collective-permute-start.18) | collective-permute-done | bytes 1572896 | tf_op jit(solution)/shard_map/ppermute | solution.py:21
  324.3 40.9 %all-reduce.1 = (f32[256]{0:T(256)S(1)}, f32[256]{0:T(256)S(1)}) all-reduce(f32[256]{0:T(256)S(1)} %get-tuple-element.12, f32[256]{0:T(256)S(1)} %get-tuple-element.11), channel_id=1, replica_groups=mesh['gx'=16,'gy'=2] {'gx','gy'}, use_global_device_ids=true, to_apply=%region_11.13 | all-reduce | flops 512 | bytes 4096 | tf_op jit(solution)/shard_map/psum | solution.py:61
  369.6 5.2 collective-permute-done.20
  374.7 4.8 collective-permute-done.21
  380.9 4.6 collective-permute-start.23
  391.3 4.1 collective-permute-start.25
  398.2 4.4 collective-permute-start.26
  404.5 7.1 collective-permute-done.26
  412.3 3.5 collective-permute-done.27
  417.2 36.8 %psum.44 = f32[256]{0:T(256)S(1)} all-reduce(f32[256]{0:T(256)S(1)} %get-tuple-element.128), channel_id=1, replica_groups=mesh['gx'=16,'gy'=2] {'gx','gy'}, use_global_device_ids=true, to_apply=%region_15.17 | all-reduce | flops 256 | bytes 2048 | tf_op jit(solution)/shard_map/psum | solution.py:61
  455.2 4.4 collective-permute-start.29
  459.6 7.0 collective-permute-done.28
  466.7 4.3 collective-permute-start.30
  478.3 24.6 %collective-permute-done.30 = f32[3,512,256]{2,1,0:T(8,128)S(1)} collective-permute-done((f32[3,512,256]{2,1,0:T(8,128)S(1)}, f32[3,512,256]{2,1,0:T(8,128)S(1)}, u32[]{:S(2)}, u32[]{:S(2)}) %collective-permute-start.30) | collective-permute-done | bytes 1572896 | tf_op jit(solution)/shard_map/ppermute | solution.py:21
  515.2 43.2 %psum.45 = f32[256]{0:T(256)S(1)} all-reduce(f32[256]{0:T(256)S(1)} %get-tuple-element.130), channel_id=1, replica_groups=mesh['gx'=16,'gy'=2] {'gx','gy'}, use_global_device_ids=true, to_apply=%region_17.19 | all-reduce | flops 256 | bytes 2048 | tf_op jit(solution)/shard_map/psum | solution.py:173
  562.8 5.2 collective-permute-done.32
  568.0 4.8 collective-permute-done.33
  574.2 4.6 collective-permute-start.35
  584.5 4.1 collective-permute-start.37
  591.4 4.4 collective-permute-start.38
  597.8 6.8 collective-permute-done.38
  609.4 36.9 %psum.46 = f32[256]{0:T(256)S(1)} all-reduce(f32[256]{0:T(256)S(1)} %get-tuple-element.132), channel_id=1, replica_groups=mesh['gx'=16,'gy'=2] {'gx','gy'}, use_global_device_ids=true, to_apply=%region_19.21 | all-reduce | flops 256 | bytes 2048 | tf_op jit(solution)/shard_map/psum | solution.py:61
  646.4 4.4 collective-permute-start.41
  650.8 7.0 collective-permute-done.40
  657.9 4.3 collective-permute-start.42
  669.3 25.0 %collective-permute-done.42 = f32[3,512,256]{2,1,0:T(8,128)S(1)} collective-permute-done((f32[3,512,256]{2,1,0:T(8,128)S(1)}, f32[3,512,256]{2,1,0:T(8,128)S(1)}, u32[]{:S(2)}, u32[]{:S(2)}) %collective-permute-start.42) | collective-permute-done | bytes 1572896 | tf_op jit(solution)/shard_map/ppermute | solution.py:21
  705.9 43.1 %psum.47 = f32[256]{0:T(256)S(1)} all-reduce(f32[256]{0:T(256)S(1)} %get-tuple-element.134), channel_id=1, replica_groups=mesh['gx'=16,'gy'=2] {'gx','gy'}, use_global_device_ids=true, to_apply=%region_21.23 | all-reduce | flops 256 | bytes 2048 | tf_op jit(solution)/shard_map/psum | solution.py:173
  (255 shorter events, 177.0 us)
Async XLA Ops:
  0.6 19.3 %copy-start = (f32[1,1,512,256]{3,2,1,0:T(8,128)S(1)}, f32[1,1,512,256]{3,2,1,0:T(8,128)}, u32[]{:S(2)}) copy-start(f32[1,1,512,256]{3,2,1,0:T(8,128)} %param.6) | copy-start | bytes 1572868
  0.7 13.4 %collective-permute-start.4 = (s32[128]{0:T(128)}, s32[128]{0:T(128)S(1)}, u32[]{:S(2)}, u32[]{:S(2)}) collective-permute-start(s32[128]{0:T(128)} %bitcast.373), channel_id=1, source_target_pairs={{0,2},{2,4},{4,6},{6,8},{8,10},{10,12},{12,14},{14,16},{16,18},{18... | collective-permute-start | bytes 1544 | tf_op jit(solution)/shard_map/ppermute | solution.py:15
  1.2 12.8 %collective-permute-start.5 = (s32[128]{0:T(128)}, s32[128]{0:T(128)S(1)}, u32[]{:S(2)}, u32[]{:S(2)}) collective-permute-start(s32[128]{0:T(128)} %bitcast.374), channel_id=1, source_target_pairs={{0,30},{2,0},{4,2},{6,4},{8,6},{10,8},{12,10},{14,12},{16,14},{18,... | collective-permute-start | bytes 1544 | tf_op jit(solution)/shard_map/ppermute | solution.py:15
  7.0 16.5 %collective-permute-start = (f32[3,512]{1,0:T(4,128)S(1)}, f32[3,512]{1,0:T(4,128)S(1)}, u32[]{:S(2)}, u32[]{:S(2)}) collective-permute-start(f32[3,512]{1,0:T(4,128)S(1)} %get-tuple-element.110), channel_id=1, source_target_pairs={{0,2},{2,4},{4,6},{6,8},{8,10},{10,12},{12,14},{14,16},{16,18},{18... | collective-permute-start | bytes 18440 | tf_op jit(solution)/shard_map/ppermute | solution.py:15
  7.0 16.4 %collective-permute-start.1 = (f32[3,512]{1,0:T(4,128)S(1)}, f32[3,512]{1,0:T(4,128)S(1)}, u32[]{:S(2)}, u32[]{:S(2)}) collective-permute-start(f32[3,512]{1,0:T(4,128)S(1)} %get-tuple-element.110), channel_id=1, source_target_pairs={{0,30},{2,0},{4,2},{6,4},{8,6},{10,8},{12,10},{14,12},{16,14},{18,... | collective-permute-start | bytes 18440 | tf_op jit(solution)/shard_map/ppermute | solution.py:15
  14.1 6.7 collective-permute-start.7
  15.4 6.3 collective-permute-start.6
  23.5 208.1 %collective-permute-start.8 = (f32[3,128,256]{2,1,0:T(8,128)}, f32[3,128,256]{2,1,0:T(8,128)}, u32[]{:S(2)}, u32[]{:S(2)}) collective-permute-start(f32[3,128,256]{2,1,0:T(8,128)} %pad_maximum_fusion.3), channel_id=1, source_target_pairs={{0,30},{2,0},{4,2},{6,4},{8,6},{10,8},{12,10},{14,12},{16,14},{18,... | collective-permute-start | bytes 1179656 | tf_op jit(solution)/shard_map/ppermute | solution.py:15
  23.5 7.5 collective-permute-start.2
  27.2 5.7 collective-permute-start.3
  29.3 202.3 %collective-permute-start.9 = (f32[3,128,256]{2,1,0:T(8,128)}, f32[3,128,256]{2,1,0:T(8,128)}, u32[]{:S(2)}, u32[]{:S(2)}) collective-permute-start(f32[3,128,256]{2,1,0:T(8,128)} %pad_maximum_fusion.4), channel_id=1, source_target_pairs={{0,2},{2,4},{4,6},{6,8},{8,10},{10,12},{12,14},{14,16},{16,18},{18... | collective-permute-start | bytes 1179656 | tf_op jit(solution)/shard_map/ppermute | solution.py:15
  170.3 54.7 %copy-start.3 = (f32[640,640]{1,0:T(8,128)S(1)}, f32[640,640]{1,0:T(8,128)}, u32[]{:S(2)}) copy-start(f32[640,640]{1,0:T(8,128)} %fusion.25) | copy-start | bytes 4915204
  232.8 11.1 %collective-permute-start.10 = (f32[128,256]{1,0:T(8,128)S(1)}, f32[128,256]{1,0:T(8,128)S(1)}, u32[]{:S(2)}, u32[]{:S(2)}) collective-permute-start(f32[128,256]{1,0:T(8,128)S(1)} %get-tuple-element.60), channel_id=1, source_target_pairs={{1,0},{3,2},{5,4},{7,6},{9,8},{11,10},{13,12},{15,14},{17,16},{19,... | collective-permute-start | bytes 393224 | tf_op jit(solution)/shard_map/ppermute | solution.py:21
  234.1 9.8 %collective-permute-start.11 = (f32[128,256]{1,0:T(8,128)S(1)}, f32[128,256]{1,0:T(8,128)S(1)}, u32[]{:S(2)}, u32[]{:S(2)}) collective-permute-start(f32[128,256]{1,0:T(8,128)S(1)} %get-tuple-element.61), channel_id=1, source_target_pairs={{0,1},{2,3},{4,5},{6,7},{8,9},{10,11},{12,13},{14,15},{16,17},{18,... | collective-permute-start | bytes 393224 | tf_op jit(solution)/shard_map/ppermute | solution.py:21
  245.7 7.1 collective-permute-start.12
  245.7 7.1 collective-permute-start.13
  252.9 6.9 collective-permute-start.14
  254.5 9.7 %collective-permute-start.15 = (f32[3,128,256]{2,1,0:T(8,128)S(1)}, f32[3,128,256]{2,1,0:T(8,128)S(1)}, u32[]{:S(2)}, u32[]{:S(2)}) collective-permute-start(f32[3,128,256]{2,1,0:T(8,128)S(1)} %pad_maximum_fusion.5), channel_id=1, source_target_pairs={{1,0},{3,2},{5,4},{7,6},{9,8},{11,10},{13,12},{15,14},{17,16},{19,... | collective-permute-start | bytes 1179656 | tf_op jit(solution)/shard_map/ppermute | solution.py:21
  264.8 11.5 %collective-permute-start.16 = (f32[512,256]{1,0:T(8,128)S(1)}, f32[512,256]{1,0:T(8,128)S(1)}, u32[]{:S(2)}, u32[]{:S(2)}) collective-permute-start(f32[512,256]{1,0:T(8,128)S(1)} %convolution_add_fusion.5), channel_id=1, source_target_pairs={{0,2},{2,4},{4,6},{6,8},{8,10},{10,12},{12,14},{14,16},{16,18},{18... | collective-permute-start | bytes 1572872 | tf_op jit(solution)/shard_map/ppermute | solution.py:15
  264.9 11.4 %collective-permute-start.17 = (f32[512,256]{1,0:T(8,128)S(1)}, f32[512,256]{1,0:T(8,128)S(1)}, u32[]{:S(2)}, u32[]{:S(2)}) collective-permute-start(f32[512,256]{1,0:T(8,128)S(1)} %convolution_add_fusion.5), channel_id=1, source_target_pairs={{0,30},{2,0},{4,2},{6,4},{8,6},{10,8},{12,10},{14,12},{16,14},{18,... | collective-permute-start | bytes 1572872 | tf_op jit(solution)/shard_map/ppermute | solution.py:15
  276.4 35.5 %collective-permute-start.18 = (f32[3,512,256]{2,1,0:T(8,128)S(1)}, f32[3,512,256]{2,1,0:T(8,128)S(1)}, u32[]{:S(2)}, u32[]{:S(2)}) collective-permute-start(f32[3,512,256]{2,1,0:T(8,128)S(1)} %pad_maximum_fusion), channel_id=1, source_target_pairs={{0,1},{2,3},{4,5},{6,7},{8,9},{10,11},{12,13},{14,15},{16,17},{18,... | collective-permute-start | bytes 4718600 | tf_op jit(solution)/shard_map/ppermute | solution.py:21
  278.0 39.5 %collective-permute-start.19 = (f32[3,512,256]{2,1,0:T(8,128)S(1)}, f32[3,512,256]{2,1,0:T(8,128)S(1)}, u32[]{:S(2)}, u32[]{:S(2)}) collective-permute-start(f32[3,512,256]{2,1,0:T(8,128)S(1)} %pad_maximum_fusion), channel_id=1, source_target_pairs={{1,0},{3,2},{5,4},{7,6},{9,8},{11,10},{13,12},{15,14},{17,16},{19,... | collective-permute-start | bytes 4718600 | tf_op jit(solution)/shard_map/ppermute | solution.py:21
  368.9 5.8 collective-permute-start.20
  369.5 10.1 %collective-permute-start.21 = (f32[3,128,256]{2,1,0:T(8,128)S(1)}, f32[3,128,256]{2,1,0:T(8,128)S(1)}, u32[]{:S(2)}, u32[]{:S(2)}) collective-permute-start(f32[3,128,256]{2,1,0:T(8,128)S(1)} %pad_maximum_fusion.7), channel_id=1, source_target_pairs={{0,2},{2,4},{4,6},{6,8},{8,10},{10,12},{12,14},{14,16},{16,18},{18... | collective-permute-start | bytes 1179656 | tf_op jit(solution)/shard_map/ppermute | solution.py:15
  379.6 7.7 %collective-permute-start.22 = (f32[128,256]{1,0:T(8,128)S(1)}, f32[128,256]{1,0:T(8,128)S(1)}, u32[]{:S(2)}, u32[]{:S(2)}) collective-permute-start(f32[128,256]{1,0:T(8,128)S(1)} %get-tuple-element.49), channel_id=1, source_target_pairs={{1,0},{3,2},{5,4},{7,6},{9,8},{11,10},{13,12},{15,14},{17,16},{19,... | collective-permute-start | bytes 393224 | tf_op jit(solution)/shard_map/ppermute | solution.py:21
  380.9 8.2 %collective-permute-start.23 = (f32[128,256]{1,0:T(8,128)S(1)}, f32[128,256]{1,0:T(8,128)S(1)}, u32[]{:S(2)}, u32[]{:S(2)}) collective-permute-start(f32[128,256]{1,0:T(8,128)S(1)} %get-tuple-element.50), channel_id=1, source_target_pairs={{0,1},{2,3},{4,5},{6,7},{8,9},{10,11},{12,13},{14,15},{16,17},{18,... | collective-permute-start | bytes 393224 | tf_op jit(solution)/shard_map/ppermute | solution.py:21
  390.9 7.2 collective-permute-start.24
  391.3 6.8 collective-permute-start.25
  398.2 13.5 %collective-permute-start.26 = (f32[3,128,256]{2,1,0:T(8,128)S(1)}, f32[3,128,256]{2,1,0:T(8,128)S(1)}, u32[]{:S(2)}, u32[]{:S(2)}) collective-permute-start(f32[3,128,256]{2,1,0:T(8,128)S(1)} %pad_maximum_fusion.8), channel_id=1, source_target_pairs={{0,1},{2,3},{4,5},{6,7},{8,9},{10,11},{12,13},{14,15},{16,17},{18,... | collective-permute-start | bytes 1179656 | tf_op jit(solution)/shard_map/ppermute | solution.py:21
  402.6 13.2 %collective-permute-start.27 = (f32[3,128,256]{2,1,0:T(8,128)S(1)}, f32[3,128,256]{2,1,0:T(8,128)S(1)}, u32[]{:S(2)}, u32[]{:S(2)}) collective-permute-start(f32[3,128,256]{2,1,0:T(8,128)S(1)} %pad_maximum_fusion.8), channel_id=1, source_target_pairs={{1,0},{3,2},{5,4},{7,6},{9,8},{11,10},{13,12},{15,14},{17,16},{19,... | collective-permute-start | bytes 1179656 | tf_op jit(solution)/shard_map/ppermute | solution.py:21
  455.1 57.2 %copy-start.1 = (f32[512,256]{1,0:T(8,128)}, f32[512,256]{1,0:T(8,128)S(1)}, u32[]{:S(2)}) copy-start(f32[512,256]{1,0:T(8,128)S(1)} %multiply_add_fusion.1) | copy-start | bytes 1572868
  455.1 11.5 %collective-permute-start.28 = (f32[512,256]{1,0:T(8,128)S(1)}, f32[512,256]{1,0:T(8,128)S(1)}, u32[]{:S(2)}, u32[]{:S(2)}) collective-permute-start(f32[512,256]{1,0:T(8,128)S(1)} %multiply_add_fusion.1), channel_id=1, source_target_pairs={{0,2},{2,4},{4,6},{6,8},{8,10},{10,12},{12,14},{14,16},{16,18},{18... | collective-permute-start | bytes 1572872 | tf_op jit(solution)/shard_map/ppermute | solution.py:15
  455.2 11.4 %collective-permute-start.29 = (f32[512,256]{1,0:T(8,128)S(1)}, f32[512,256]{1,0:T(8,128)S(1)}, u32[]{:S(2)}, u32[]{:S(2)}) collective-permute-start(f32[512,256]{1,0:T(8,128)S(1)} %multiply_add_fusion.1), channel_id=1, source_target_pairs={{0,30},{2,0},{4,2},{6,4},{8,6},{10,8},{12,10},{14,12},{16,14},{18,... | collective-permute-start | bytes 1572872 | tf_op jit(solution)/shard_map/ppermute | solution.py:15
  466.7 36.1 %collective-permute-start.30 = (f32[3,512,256]{2,1,0:T(8,128)S(1)}, f32[3,512,256]{2,1,0:T(8,128)S(1)}, u32[]{:S(2)}, u32[]{:S(2)}) collective-permute-start(f32[3,512,256]{2,1,0:T(8,128)S(1)} %pad_maximum_fusion.1), channel_id=1, source_target_pairs={{0,1},{2,3},{4,5},{6,7},{8,9},{10,11},{12,13},{14,15},{16,17},{18,... | collective-permute-start | bytes 4718600 | tf_op jit(solution)/shard_map/ppermute | solution.py:21
  471.0 37.4 %collective-permute-start.31 = (f32[3,512,256]{2,1,0:T(8,128)S(1)}, f32[3,512,256]{2,1,0:T(8,128)S(1)}, u32[]{:S(2)}, u32[]{:S(2)}) collective-permute-start(f32[3,512,256]{2,1,0:T(8,128)S(1)} %pad_maximum_fusion.1), channel_id=1, source_target_pairs={{1,0},{3,2},{5,4},{7,6},{9,8},{11,10},{13,12},{15,14},{17,16},{19,... | collective-permute-start | bytes 4718600 | tf_op jit(solution)/shard_map/ppermute | solution.py:21
  562.1 5.9 collective-permute-start.32
  562.7 10.1 %collective-permute-start.33 = (f32[3,128,256]{2,1,0:T(8,128)S(1)}, f32[3,128,256]{2,1,0:T(8,128)S(1)}, u32[]{:S(2)}, u32[]{:S(2)}) collective-permute-start(f32[3,128,256]{2,1,0:T(8,128)S(1)} %pad_maximum_fusion.10), channel_id=1, source_target_pairs={{0,2},{2,4},{4,6},{6,8},{8,10},{10,12},{12,14},{14,16},{16,18},{18... | collective-permute-start | bytes 1179656 | tf_op jit(solution)/shard_map/ppermute | solution.py:15
  572.9 7.8 %collective-permute-start.34 = (f32[128,256]{1,0:T(8,128)S(1)}, f32[128,256]{1,0:T(8,128)S(1)}, u32[]{:S(2)}, u32[]{:S(2)}) collective-permute-start(f32[128,256]{1,0:T(8,128)S(1)} %get-tuple-element.38), channel_id=1, source_target_pairs={{1,0},{3,2},{5,4},{7,6},{9,8},{11,10},{13,12},{15,14},{17,16},{19,... | collective-permute-start | bytes 393224 | tf_op jit(solution)/shard_map/ppermute | solution.py:21
  574.2 8.2 %collective-permute-start.35 = (f32[128,256]{1,0:T(8,128)S(1)}, f32[128,256]{1,0:T(8,128)S(1)}, u32[]{:S(2)}, u32[]{:S(2)}) collective-permute-start(f32[128,256]{1,0:T(8,128)S(1)} %get-tuple-element.39), channel_id=1, source_target_pairs={{0,1},{2,3},{4,5},{6,7},{8,9},{10,11},{12,13},{14,15},{16,17},{18,... | collective-permute-start | bytes 393224 | tf_op jit(solution)/shard_map/ppermute | solution.py:21
  584.2 7.2 collective-permute-start.36
  584.5 6.9 collective-permute-start.37
  591.4 13.1 %collective-permute-start.38 = (f32[3,128,256]{2,1,0:T(8,128)S(1)}, f32[3,128,256]{2,1,0:T(8,128)S(1)}, u32[]{:S(2)}, u32[]{:S(2)}) collective-permute-start(f32[3,128,256]{2,1,0:T(8,128)S(1)} %pad_maximum_fusion.11), channel_id=1, source_target_pairs={{0,1},{2,3},{4,5},{6,7},{8,9},{10,11},{12,13},{14,15},{16,17},{18,... | collective-permute-start | bytes 1179656 | tf_op jit(solution)/shard_map/ppermute | solution.py:21
  595.9 12.8 %collective-permute-start.39 = (f32[3,128,256]{2,1,0:T(8,128)S(1)}, f32[3,128,256]{2,1,0:T(8,128)S(1)}, u32[]{:S(2)}, u32[]{:S(2)}) collective-permute-start(f32[3,128,256]{2,1,0:T(8,128)S(1)} %pad_maximum_fusion.11), channel_id=1, source_target_pairs={{1,0},{3,2},{5,4},{7,6},{9,8},{11,10},{13,12},{15,14},{17,16},{19,... | collective-permute-start | bytes 1179656 | tf_op jit(solution)/shard_map/ppermute | solution.py:21
  605.2 41.1 %copy-start.2 = (f32[512,256]{1,0:T(8,128)S(1)}, f32[512,256]{1,0:T(8,128)}, u32[]{:S(2)}) copy-start(f32[512,256]{1,0:T(8,128)} %copy-done.1) | copy-start | bytes 1572868
  646.3 11.5 %collective-permute-start.40 = (f32[512,256]{1,0:T(8,128)S(1)}, f32[512,256]{1,0:T(8,128)S(1)}, u32[]{:S(2)}, u32[]{:S(2)}) collective-permute-start(f32[512,256]{1,0:T(8,128)S(1)} %multiply_add_fusion), channel_id=1, source_target_pairs={{0,2},{2,4},{4,6},{6,8},{8,10},{10,12},{12,14},{14,16},{16,18},{18... | collective-permute-start | bytes 1572872 | tf_op jit(solution)/shard_map/ppermute | solution.py:15
  646.4 11.4 %collective-permute-start.41 = (f32[512,256]{1,0:T(8,128)S(1)}, f32[512,256]{1,0:T(8,128)S(1)}, u32[]{:S(2)}, u32[]{:S(2)}) collective-permute-start(f32[512,256]{1,0:T(8,128)S(1)} %multiply_add_fusion), channel_id=1, source_target_pairs={{0,30},{2,0},{4,2},{6,4},{8,6},{10,8},{12,10},{14,12},{16,14},{18,... | collective-permute-start | bytes 1572872 | tf_op jit(solution)/shard_map/ppermute | solution.py:15
  657.9 36.3 %collective-permute-start.42 = (f32[3,512,256]{2,1,0:T(8,128)S(1)}, f32[3,512,256]{2,1,0:T(8,128)S(1)}, u32[]{:S(2)}, u32[]{:S(2)}) collective-permute-start(f32[3,512,256]{2,1,0:T(8,128)S(1)} %pad_maximum_fusion.2), channel_id=1, source_target_pairs={{0,1},{2,3},{4,5},{6,7},{8,9},{10,11},{12,13},{14,15},{16,17},{18,... | collective-permute-start | bytes 4718600 | tf_op jit(solution)/shard_map/ppermute | solution.py:21
  662.2 37.6 %collective-permute-start.43 = (f32[3,512,256]{2,1,0:T(8,128)S(1)}, f32[3,512,256]{2,1,0:T(8,128)S(1)}, u32[]{:S(2)}, u32[]{:S(2)}) collective-permute-start(f32[3,512,256]{2,1,0:T(8,128)S(1)} %pad_maximum_fusion.2), channel_id=1, source_target_pairs={{1,0},{3,2},{5,4},{7,6},{9,8},{11,10},{13,12},{15,14},{17,16},{19,... | collective-permute-start | bytes 4718600 | tf_op jit(solution)/shard_map/ppermute | solution.py:21
  (5 other events, 28.6 us)
where the time goes:
time: 756 us; the launch traced here: 751 us
  blocking collectives  201 us (27%)
  other arithmetic  168 us (22%)
  waiting for transfers between devices  161 us (21%)
  starting transfers between devices  96.9 us (13%)
  matrix products  94.8 us (13%)
  local copies, waits for them, and re-layouts  22.5 us (3%)
    psum x3, blocking collectives, residual_dot(): return lax.psum(column_sum(residue, precond), ('gx', 'gy'))  115 us
    ppermute x22, waiting for transfers between devices, passed_along(): return lax.ppermute(block, axis, route)  112 us
    another operation x19, other arithmetic, shards(): factor = jnp.linalg.cholesky(local_matrix)  101 us
    psum x2, blocking collectives, shards(): lax.psum(column_sum(direction, accumulated), ('gx', 'gy'))  86.3 us
    ppermute x22, starting transfers between devices, passed_along(): return lax.ppermute(block, axis, route)  57.9 us
    dot_general x27, matrix products, shards(): jnp.dot(kernel_block(own_pos, positions[operate_row_off][operate_col_off]...  52.9 us
    another operation x3, other arithmetic, shards(): lax.linalg.triangular_solve(factor, jnp.eye(ext_len, dtype=jnp.float32),...  52 us
    ppermute x22, waiting for transfers between devices, shifted(): lax.ppermute(value, axis, [(i, (i + by) % count) for i in range(count)])  49 us
  transfers between devices with their start and end apart: 44, of which 24 were waited for; matrix products, arithmetic and copies ran while one was open for 33% of the time, Pallas kernels for 0%

commit v1 on v0

--- a/solution.py
+++ b/solution.py
@@ -58,7 +58,7 @@
 
 
 def residual_dot(residue, precond):
-    return lax.psum(column_sum(residue, precond), ("gx", "gy"))
+    return jnp.sum(lax.all_gather(column_sum(residue, precond), ("gx", "gy")), axis=0)
 
 
 def shards(right_side, coords, noise, intersect):

time: 756 us -> 864 us (1.14)
  blocking collectives: 201 us -> 309 us
    all_gather x0 -> x3, blocking collectives: none -> 198 us  [residual_dot(): lax.all_gather(column_sum(residue, precond), ('gx', 'gy'))]
    psum x3 -> x0, blocking collectives: 115 us -> none  [residual_dot(): return lax.psum(column_sum(residue, precond), ('gx', 'gy'))]
    psum x2 -> x3, blocking collectives: 86.3 us -> 111 us  [shards(): lax.psum(column_sum(direction, accumulated), ('gx', 'gy'))]
  transfers between devices with their start and end apart: 44 -> 44, of which waited for: 24 -> 24; matrix products, arithmetic and copies ran while one was open for 33% -> 29% of each run, Pallas kernels for 0% -> 0%
where the time goes in v1:
time: 864 us; the launch traced here: 858 us
  blocking collectives  309 us (36%)
  other arithmetic  168 us (19%)
  waiting for transfers between devices  158 us (18%)
  starting transfers between devices  98.1 us (11%)
  matrix products  94.8 us (11%)
  local copies, waits for them, and re-layouts  23 us (3%)
    all_gather x3, blocking collectives, residual_dot(): lax.all_gather(column_sum(residue, precond), ('gx', 'gy'))  198 us
    psum x3, blocking collectives, shards(): lax.psum(column_sum(direction, accumulated), ('gx', 'gy'))  111 us
    ppermute x22, waiting for transfers between devices, passed_along(): return lax.ppermute(block, axis, route)  109 us
    another operation x19, other arithmetic, shards(): factor = jnp.linalg.cholesky(local_matrix)  102 us
    ppermute x22, starting transfers between devices, passed_along(): return lax.ppermute(block, axis, route)  55.8 us
    dot_general x27, matrix products, shards(): jnp.dot(kernel_block(own_pos, positions[operate_row_off][operate_col_off]...  52.9 us
    another operation x3, other arithmetic, shards(): lax.linalg.triangular_solve(factor, jnp.eye(ext_len, dtype=jnp.float32),...  52 us
    ppermute x22, waiting for transfers between devices, shifted(): lax.ppermute(value, axis, [(i, (i + by) % count) for i in range(count)])  48.8 us
  transfers between devices with their start and end apart: 44, of which 24 were waited for; matrix products, arithmetic and copies ran while one was open for 29% of the time, Pallas kernels for 0%

profile of v1, /device:TPU:0, one launch (start us, length us, event | category | flops | bytes accessed | tf_op | source)
XLA Modules:
  0.0 857.5 jit_solution(15242717837358744038)
XLA Ops:
  1.2 5.0 collective-permute-start.5
  7.0 4.4 collective-permute-start.1
  15.4 4.5 collective-permute-start.6
  23.5 3.7 collective-permute-start.2
  38.7 11.7 %cholesky.132 = f32[128,128]{1,0:T(8,128)S(1)} custom-call(f32[128,128]{1,0:T(8,128)S(1)} %cholesky.337), custom_call_target="Cholesky" | custom-call | tf_op jit(solution)/shard_map/jit(cholesky)/cholesky | solution.py:108
  50.6 9.8 %custom-call.38 = f32[1,128,128]{1,2,0:T(8,128)S(1)} custom-call(f32[1,128,128]{2,1,0:T(8,128)S(1)} %get-tuple-element.81), custom_call_target="InvertDiagBlocksLowerTriangular" | custom-call | tf_op jit(solution)/shard_map/jit(cholesky)/cholesky | solution.py:108
  63.0 11.9 %cholesky.270 = f32[128,128]{1,0:T(8,128)S(1)} custom-call(f32[128,128]{1,0:T(8,128)S(1)} %cholesky.341), custom_call_target="Cholesky" | custom-call | tf_op jit(solution)/shard_map/jit(cholesky)/cholesky | solution.py:108
  76.3 9.8 %custom-call.39 = f32[1,128,128]{1,2,0:T(8,128)S(1)} custom-call(f32[1,128,128]{2,1,0:T(8,128)S(1)} %get-tuple-element.78), custom_call_target="InvertDiagBlocksLowerTriangular" | custom-call | tf_op jit(solution)/shard_map/jit(cholesky)/cholesky | solution.py:108
  87.9 11.7 %cholesky.291 = f32[128,128]{1,0:T(8,128)S(1)} custom-call(f32[128,128]{1,0:T(8,128)S(1)} %cholesky.346), custom_call_target="Cholesky" | custom-call | tf_op jit(solution)/shard_map/jit(cholesky)/cholesky | solution.py:108
  100.4 9.8 %custom-call.40 = f32[1,128,128]{1,2,0:T(8,128)S(1)} custom-call(f32[1,128,128]{2,1,0:T(8,128)S(1)} %get-tuple-element.75), custom_call_target="InvertDiagBlocksLowerTriangular" | custom-call | tf_op jit(solution)/shard_map/jit(cholesky)/cholesky | solution.py:108
  112.1 11.7 %cholesky.310 = f32[128,128]{1,0:T(8,128)S(1)} custom-call(f32[128,128]{1,0:T(8,128)S(1)} %cholesky.351), custom_call_target="Cholesky" | custom-call | tf_op jit(solution)/shard_map/jit(cholesky)/cholesky | solution.py:108
  124.4 9.8 %custom-call.41 = f32[1,128,128]{1,2,0:T(8,128)S(1)} custom-call(f32[1,128,128]{2,1,0:T(8,128)S(1)} %get-tuple-element.72), custom_call_target="InvertDiagBlocksLowerTriangular" | custom-call | tf_op jit(solution)/shard_map/jit(cholesky)/cholesky | solution.py:108
  135.7 11.7 %cholesky.327 = f32[128,128]{1,0:T(8,128)S(1)} custom-call(f32[128,128]{1,0:T(8,128)S(1)} %convolution_subtract_fusion.6), custom_call_target="Cholesky" | custom-call | tf_op jit(solution)/shard_map/jit(cholesky)/cholesky | solution.py:108
  152.7 18.3 %while.1 = (s32[]{:T(128)}, f32[640,640]{1,0:T(8,128)}, s32[5,2]{0,1:T(2,128)S(1)}, f32[5,128,128]{2,1,0:T(8,128)}, s32[]{:T(128)}) while((s32[]{:T(128)}, f32[640,640]{1,0:T(8,128)}, s32[5,2]{0,1:T(2,128)S(1)}, f32[5,128,128]{2,1,0:T(8,128)}, s32[]{:T(128)}) %tuple.96), condition=%wide.while_cond, body=%wide.while_body.sunk | while | flops 2 | bytes 132705 | solution.py:109
  171.0 50.7 %custom-call.42 = f32[5,128,128]{1,2,0:T(8,128)} custom-call(f32[5,128,128]{2,1,0:T(8,128)} %get-tuple-element.10), custom_call_target="InvertDiagBlocksLowerTriangular" | custom-call | tf_op jit(solution)/shard_map/triangular_solve | solution.py:109
  234.8 4.7 collective-permute-start.11
  239.5 5.0 fusion.240
  246.4 4.4 collective-permute-start.13
  261.0 3.8 collective-permute-done.15
  265.5 4.4 collective-permute-start.17
  270.0 6.9 collective-permute-done.16
  286.0 26.6 %collective-permute-done.18 = f32[3,512,256]{2,1,0:T(8,128)S(1)} collective-permute-done((f32[3,512,256]{2,1,0:T(8,128)S(1)}, f32[3,512,256]{2,1,0:T(8,128)S(1)}, u32[]{:S(2)}, u32[]{:S(2)}) %collective-permute-start.18) | collective-permute-done | bytes 1572896 | tf_op jit(solution)/shard_map/ppermute | solution.py:21
  324.9 68.8 %all-gather.3 = f32[32,1,256]{2,1,0:T(1,128)S(1)} all-gather(f32[1,1,256]{2,1,0:T(1,128)S(1)} %bitcast.495), channel_id=2, replica_groups=mesh['gx'=16,'gy'=2] {'gx','gy'}, dimensions={0}, use_global_device_ids=true | all-gather | bytes 33792 | tf_op jit(solution)/shard_map/all_gather | solution.py:61
  393.8 36.8 %psum.21 = f32[256]{0:T(256)S(1)} all-reduce(f32[256]{0:T(256)S(1)} %get-tuple-element.11), channel_id=1, replica_groups=mesh['gx'=16,'gy'=2] {'gx','gy'}, use_global_device_ids=true, to_apply=%region_13.15 | all-reduce | flops 256 | bytes 2048 | tf_op jit(solution)/shard_map/psum | solution.py:173
  435.7 5.2 collective-permute-done.20
  440.9 4.8 collective-permute-done.21
  447.1 4.6 collective-permute-start.23
  456.9 4.4 collective-permute-start.25
  464.1 4.4 collective-permute-start.26
  470.5 6.9 collective-permute-done.26
  477.9 3.5 collective-permute-done.27
  482.9 63.6 %all-gather.4 = f32[32,1,256]{2,1,0:T(1,128)S(1)} all-gather(f32[1,1,256]{2,1,0:T(1,128)S(1)} %bitcast.386), channel_id=3, replica_groups=mesh['gx'=16,'gy'=2] {'gx','gy'}, dimensions={0}, use_global_device_ids=true | all-gather | bytes 33792 | tf_op jit(solution)/shard_map/all_gather | solution.py:61
  547.7 4.4 collective-permute-start.29
  552.1 7.0 collective-permute-done.28
  559.2 4.1 collective-permute-start.30
  570.6 24.3 %collective-permute-done.30 = f32[3,512,256]{2,1,0:T(8,128)S(1)} collective-permute-done((f32[3,512,256]{2,1,0:T(8,128)S(1)}, f32[3,512,256]{2,1,0:T(8,128)S(1)}, u32[]{:S(2)}, u32[]{:S(2)}) %collective-permute-start.30) | collective-permute-done | bytes 1572896 | tf_op jit(solution)/shard_map/ppermute | solution.py:21
  607.2 37.3 %psum.22 = f32[256]{0:T(256)S(1)} all-reduce(f32[256]{0:T(256)S(1)} %get-tuple-element.128), channel_id=1, replica_groups=mesh['gx'=16,'gy'=2] {'gx','gy'}, use_global_device_ids=true, to_apply=%region_17.19 | all-reduce | flops 256 | bytes 2048 | tf_op jit(solution)/shard_map/psum | solution.py:173
  651.5 5.2 collective-permute-done.32
  656.7 4.7 collective-permute-done.33
  662.8 4.6 collective-permute-start.35
  671.7 4.4 collective-permute-start.37
  678.8 4.4 collective-permute-start.38
  685.1 4.7 collective-permute-done.38
  694.6 65.2 %all-gather.5 = f32[32,1,256]{2,1,0:T(1,128)S(1)} all-gather(f32[1,1,256]{2,1,0:T(1,128)S(1)} %bitcast.385), channel_id=4, replica_groups=mesh['gx'=16,'gy'=2] {'gx','gy'}, dimensions={0}, use_global_device_ids=true | all-gather | bytes 33792 | tf_op jit(solution)/shard_map/all_gather | solution.py:61
  760.1 4.4 collective-permute-start.41
  764.5 7.0 collective-permute-done.40
  781.1 25.9 %collective-permute-done.42 = f32[3,512,256]{2,1,0:T(8,128)S(1)} collective-permute-done((f32[3,512,256]{2,1,0:T(8,128)S(1)}, f32[3,512,256]{2,1,0:T(8,128)S(1)}, u32[]{:S(2)}, u32[]{:S(2)}) %collective-permute-start.42) | collective-permute-done | bytes 1572896 | tf_op jit(solution)/shard_map/ppermute | solution.py:21
  818.6 37.3 %psum.23 = f32[256]{0:T(256)S(1)} all-reduce(f32[256]{0:T(256)S(1)} %get-tuple-element.132), channel_id=1, replica_groups=mesh['gx'=16,'gy'=2] {'gx','gy'}, use_global_device_ids=true, to_apply=%region_21.23 | all-reduce | flops 256 | bytes 2048 | tf_op jit(solution)/shard_map/psum | solution.py:173
  (259 shorter events, 181.3 us)
Async XLA Ops:
  0.6 19.3 %copy-start = (f32[1,1,512,256]{3,2,1,0:T(8,128)S(1)}, f32[1,1,512,256]{3,2,1,0:T(8,128)}, u32[]{:S(2)}) copy-start(f32[1,1,512,256]{3,2,1,0:T(8,128)} %param.6) | copy-start | bytes 1572868
  0.7 13.4 %collective-permute-start.4 = (s32[128]{0:T(128)}, s32[128]{0:T(128)S(1)}, u32[]{:S(2)}, u32[]{:S(2)}) collective-permute-start(s32[128]{0:T(128)} %bitcast.376), channel_id=1, source_target_pairs={{0,2},{2,4},{4,6},{6,8},{8,10},{10,12},{12,14},{14,16},{16,18},{18... | collective-permute-start | bytes 1544 | tf_op jit(solution)/shard_map/ppermute | solution.py:15
  1.2 12.8 %collective-permute-start.5 = (s32[128]{0:T(128)}, s32[128]{0:T(128)S(1)}, u32[]{:S(2)}, u32[]{:S(2)}) collective-permute-start(s32[128]{0:T(128)} %bitcast.377), channel_id=1, source_target_pairs={{0,30},{2,0},{4,2},{6,4},{8,6},{10,8},{12,10},{14,12},{16,14},{18,... | collective-permute-start | bytes 1544 | tf_op jit(solution)/shard_map/ppermute | solution.py:15
  7.0 16.5 %collective-permute-start = (f32[3,512]{1,0:T(4,128)S(1)}, f32[3,512]{1,0:T(4,128)S(1)}, u32[]{:S(2)}, u32[]{:S(2)}) collective-permute-start(f32[3,512]{1,0:T(4,128)S(1)} %get-tuple-element.108), channel_id=1, source_target_pairs={{0,2},{2,4},{4,6},{6,8},{8,10},{10,12},{12,14},{14,16},{16,18},{18... | collective-permute-start | bytes 18440 | tf_op jit(solution)/shard_map/ppermute | solution.py:15
  7.0 16.4 %collective-permute-start.1 = (f32[3,512]{1,0:T(4,128)S(1)}, f32[3,512]{1,0:T(4,128)S(1)}, u32[]{:S(2)}, u32[]{:S(2)}) collective-permute-start(f32[3,512]{1,0:T(4,128)S(1)} %get-tuple-element.108), channel_id=1, source_target_pairs={{0,30},{2,0},{4,2},{6,4},{8,6},{10,8},{12,10},{14,12},{16,14},{18,... | collective-permute-start | bytes 18440 | tf_op jit(solution)/shard_map/ppermute | solution.py:15
  14.1 6.7 collective-permute-start.7
  15.4 6.3 collective-permute-start.6
  23.5 208.8 %collective-permute-start.8 = (f32[3,128,256]{2,1,0:T(8,128)}, f32[3,128,256]{2,1,0:T(8,128)}, u32[]{:S(2)}, u32[]{:S(2)}) collective-permute-start(f32[3,128,256]{2,1,0:T(8,128)} %pad_maximum_fusion.3), channel_id=1, source_target_pairs={{0,30},{2,0},{4,2},{6,4},{8,6},{10,8},{12,10},{14,12},{16,14},{18,... | collective-permute-start | bytes 1179656 | tf_op jit(solution)/shard_map/ppermute | solution.py:15
  23.5 7.5 collective-permute-start.2
  27.2 5.7 collective-permute-start.3
  29.3 202.9 %collective-permute-start.9 = (f32[3,128,256]{2,1,0:T(8,128)}, f32[3,128,256]{2,1,0:T(8,128)}, u32[]{:S(2)}, u32[]{:S(2)}) collective-permute-start(f32[3,128,256]{2,1,0:T(8,128)} %pad_maximum_fusion.4), channel_id=1, source_target_pairs={{0,2},{2,4},{4,6},{6,8},{8,10},{10,12},{12,14},{14,16},{16,18},{18... | collective-permute-start | bytes 1179656 | tf_op jit(solution)/shard_map/ppermute | solution.py:15
  171.0 54.7 %copy-start.3 = (f32[640,640]{1,0:T(8,128)S(1)}, f32[640,640]{1,0:T(8,128)}, u32[]{:S(2)}) copy-start(f32[640,640]{1,0:T(8,128)} %fusion.25) | copy-start | bytes 4915204
  233.5 11.1 %collective-permute-start.10 = (f32[128,256]{1,0:T(8,128)S(1)}, f32[128,256]{1,0:T(8,128)S(1)}, u32[]{:S(2)}, u32[]{:S(2)}) collective-permute-start(f32[128,256]{1,0:T(8,128)S(1)} %get-tuple-element.58), channel_id=1, source_target_pairs={{1,0},{3,2},{5,4},{7,6},{9,8},{11,10},{13,12},{15,14},{17,16},{19,... | collective-permute-start | bytes 393224 | tf_op jit(solution)/shard_map/ppermute | solution.py:21
  234.8 9.8 %collective-permute-start.11 = (f32[128,256]{1,0:T(8,128)S(1)}, f32[128,256]{1,0:T(8,128)S(1)}, u32[]{:S(2)}, u32[]{:S(2)}) collective-permute-start(f32[128,256]{1,0:T(8,128)S(1)} %get-tuple-element.59), channel_id=1, source_target_pairs={{0,1},{2,3},{4,5},{6,7},{8,9},{10,11},{12,13},{14,15},{16,17},{18,... | collective-permute-start | bytes 393224 | tf_op jit(solution)/shard_map/ppermute | solution.py:21
  246.4 7.1 collective-permute-start.12
  246.4 7.1 collective-permute-start.13
  253.5 6.9 collective-permute-start.14
  255.2 9.7 %collective-permute-start.15 = (f32[3,128,256]{2,1,0:T(8,128)S(1)}, f32[3,128,256]{2,1,0:T(8,128)S(1)}, u32[]{:S(2)}, u32[]{:S(2)}) collective-permute-start(f32[3,128,256]{2,1,0:T(8,128)S(1)} %pad_maximum_fusion.5), channel_id=1, source_target_pairs={{1,0},{3,2},{5,4},{7,6},{9,8},{11,10},{13,12},{15,14},{17,16},{19,... | collective-permute-start | bytes 1179656 | tf_op jit(solution)/shard_map/ppermute | solution.py:21
  265.5 11.5 %collective-permute-start.16 = (f32[512,256]{1,0:T(8,128)S(1)}, f32[512,256]{1,0:T(8,128)S(1)}, u32[]{:S(2)}, u32[]{:S(2)}) collective-permute-start(f32[512,256]{1,0:T(8,128)S(1)} %convolution_add_fusion.5), channel_id=1, source_target_pairs={{0,2},{2,4},{4,6},{6,8},{8,10},{10,12},{12,14},{14,16},{16,18},{18... | collective-permute-start | bytes 1572872 | tf_op jit(solution)/shard_map/ppermute | solution.py:15
  265.5 11.4 %collective-permute-start.17 = (f32[512,256]{1,0:T(8,128)S(1)}, f32[512,256]{1,0:T(8,128)S(1)}, u32[]{:S(2)}, u32[]{:S(2)}) collective-permute-start(f32[512,256]{1,0:T(8,128)S(1)} %convolution_add_fusion.5), channel_id=1, source_target_pairs={{0,30},{2,0},{4,2},{6,4},{8,6},{10,8},{12,10},{14,12},{16,14},{18,... | collective-permute-start | bytes 1572872 | tf_op jit(solution)/shard_map/ppermute | solution.py:15
  277.1 35.5 %collective-permute-start.18 = (f32[3,512,256]{2,1,0:T(8,128)S(1)}, f32[3,512,256]{2,1,0:T(8,128)S(1)}, u32[]{:S(2)}, u32[]{:S(2)}) collective-permute-start(f32[3,512,256]{2,1,0:T(8,128)S(1)} %pad_maximum_fusion), channel_id=1, source_target_pairs={{0,1},{2,3},{4,5},{6,7},{8,9},{10,11},{12,13},{14,15},{16,17},{18,... | collective-permute-start | bytes 4718600 | tf_op jit(solution)/shard_map/ppermute | solution.py:21
  278.7 39.5 %collective-permute-start.19 = (f32[3,512,256]{2,1,0:T(8,128)S(1)}, f32[3,512,256]{2,1,0:T(8,128)S(1)}, u32[]{:S(2)}, u32[]{:S(2)}) collective-permute-start(f32[3,512,256]{2,1,0:T(8,128)S(1)} %pad_maximum_fusion), channel_id=1, source_target_pairs={{1,0},{3,2},{5,4},{7,6},{9,8},{11,10},{13,12},{15,14},{17,16},{19,... | collective-permute-start | bytes 4718600 | tf_op jit(solution)/shard_map/ppermute | solution.py:21
  434.4 6.5 collective-permute-start.20
  435.6 10.1 %collective-permute-start.21 = (f32[3,128,256]{2,1,0:T(8,128)S(1)}, f32[3,128,256]{2,1,0:T(8,128)S(1)}, u32[]{:S(2)}, u32[]{:S(2)}) collective-permute-start(f32[3,128,256]{2,1,0:T(8,128)S(1)} %pad_maximum_fusion.7), channel_id=1, source_target_pairs={{0,2},{2,4},{4,6},{6,8},{8,10},{10,12},{12,14},{14,16},{16,18},{18... | collective-permute-start | bytes 1179656 | tf_op jit(solution)/shard_map/ppermute | solution.py:15
  445.8 8.1 collective-permute-start.22
  447.1 8.0 collective-permute-start.23
  456.8 7.2 collective-permute-start.24
  456.9 7.2 collective-permute-start.25
  464.1 13.2 %collective-permute-start.26 = (f32[3,128,256]{2,1,0:T(8,128)S(1)}, f32[3,128,256]{2,1,0:T(8,128)S(1)}, u32[]{:S(2)}, u32[]{:S(2)}) collective-permute-start(f32[3,128,256]{2,1,0:T(8,128)S(1)} %pad_maximum_fusion.8), channel_id=1, source_target_pairs={{0,1},{2,3},{4,5},{6,7},{8,9},{10,11},{12,13},{14,15},{16,17},{18,... | collective-permute-start | bytes 1179656 | tf_op jit(solution)/shard_map/ppermute | solution.py:21
  468.5 12.9 %collective-permute-start.27 = (f32[3,128,256]{2,1,0:T(8,128)S(1)}, f32[3,128,256]{2,1,0:T(8,128)S(1)}, u32[]{:S(2)}, u32[]{:S(2)}) collective-permute-start(f32[3,128,256]{2,1,0:T(8,128)S(1)} %pad_maximum_fusion.8), channel_id=1, source_target_pairs={{1,0},{3,2},{5,4},{7,6},{9,8},{11,10},{13,12},{15,14},{17,16},{19,... | collective-permute-start | bytes 1179656 | tf_op jit(solution)/shard_map/ppermute | solution.py:21
  547.6 56.7 %copy-start.1 = (f32[512,256]{1,0:T(8,128)}, f32[512,256]{1,0:T(8,128)S(1)}, u32[]{:S(2)}) copy-start(f32[512,256]{1,0:T(8,128)S(1)} %multiply_add_fusion.1) | copy-start | bytes 1572868
  547.6 11.5 %collective-permute-start.28 = (f32[512,256]{1,0:T(8,128)S(1)}, f32[512,256]{1,0:T(8,128)S(1)}, u32[]{:S(2)}, u32[]{:S(2)}) collective-permute-start(f32[512,256]{1,0:T(8,128)S(1)} %multiply_add_fusion.1), channel_id=1, source_target_pairs={{0,2},{2,4},{4,6},{6,8},{8,10},{10,12},{12,14},{14,16},{16,18},{18... | collective-permute-start | bytes 1572872 | tf_op jit(solution)/shard_map/ppermute | solution.py:15
  547.7 11.4 %collective-permute-start.29 = (f32[512,256]{1,0:T(8,128)S(1)}, f32[512,256]{1,0:T(8,128)S(1)}, u32[]{:S(2)}, u32[]{:S(2)}) collective-permute-start(f32[512,256]{1,0:T(8,128)S(1)} %multiply_add_fusion.1), channel_id=1, source_target_pairs={{0,30},{2,0},{4,2},{6,4},{8,6},{10,8},{12,10},{14,12},{16,14},{18,... | collective-permute-start | bytes 1572872 | tf_op jit(solution)/shard_map/ppermute | solution.py:15
  559.2 35.6 %collective-permute-start.30 = (f32[3,512,256]{2,1,0:T(8,128)S(1)}, f32[3,512,256]{2,1,0:T(8,128)S(1)}, u32[]{:S(2)}, u32[]{:S(2)}) collective-permute-start(f32[3,512,256]{2,1,0:T(8,128)S(1)} %pad_maximum_fusion.1), channel_id=1, source_target_pairs={{0,1},{2,3},{4,5},{6,7},{8,9},{10,11},{12,13},{14,15},{16,17},{18,... | collective-permute-start | bytes 4718600 | tf_op jit(solution)/shard_map/ppermute | solution.py:21
  563.3 37.1 %collective-permute-start.31 = (f32[3,512,256]{2,1,0:T(8,128)S(1)}, f32[3,512,256]{2,1,0:T(8,128)S(1)}, u32[]{:S(2)}, u32[]{:S(2)}) collective-permute-start(f32[3,512,256]{2,1,0:T(8,128)S(1)} %pad_maximum_fusion.1), channel_id=1, source_target_pairs={{1,0},{3,2},{5,4},{7,6},{9,8},{11,10},{13,12},{15,14},{17,16},{19,... | collective-permute-start | bytes 4718600 | tf_op jit(solution)/shard_map/ppermute | solution.py:21
  648.2 8.5 collective-permute-start.32
  651.4 10.0 %collective-permute-start.33 = (f32[3,128,256]{2,1,0:T(8,128)S(1)}, f32[3,128,256]{2,1,0:T(8,128)S(1)}, u32[]{:S(2)}, u32[]{:S(2)}) collective-permute-start(f32[3,128,256]{2,1,0:T(8,128)S(1)} %pad_maximum_fusion.10), channel_id=1, source_target_pairs={{0,2},{2,4},{4,6},{6,8},{8,10},{10,12},{12,14},{14,16},{16,18},{18... | collective-permute-start | bytes 1179656 | tf_op jit(solution)/shard_map/ppermute | solution.py:15
  661.5 6.9 collective-permute-start.34
  662.8 7.1 collective-permute-start.35
  671.6 7.1 collective-permute-start.36
  671.7 7.1 collective-permute-start.37
  678.8 11.0 %collective-permute-start.38 = (f32[3,128,256]{2,1,0:T(8,128)S(1)}, f32[3,128,256]{2,1,0:T(8,128)S(1)}, u32[]{:S(2)}, u32[]{:S(2)}) collective-permute-start(f32[3,128,256]{2,1,0:T(8,128)S(1)} %pad_maximum_fusion.11), channel_id=1, source_target_pairs={{0,1},{2,3},{4,5},{6,7},{8,9},{10,11},{12,13},{14,15},{16,17},{18,... | collective-permute-start | bytes 1179656 | tf_op jit(solution)/shard_map/ppermute | solution.py:21
  683.2 10.7 %collective-permute-start.39 = (f32[3,128,256]{2,1,0:T(8,128)S(1)}, f32[3,128,256]{2,1,0:T(8,128)S(1)}, u32[]{:S(2)}, u32[]{:S(2)}) collective-permute-start(f32[3,128,256]{2,1,0:T(8,128)S(1)} %pad_maximum_fusion.11), channel_id=1, source_target_pairs={{1,0},{3,2},{5,4},{7,6},{9,8},{11,10},{13,12},{15,14},{17,16},{19,... | collective-permute-start | bytes 1179656 | tf_op jit(solution)/shard_map/ppermute | solution.py:21
  690.4 69.5 %copy-start.2 = (f32[512,256]{1,0:T(8,128)S(1)}, f32[512,256]{1,0:T(8,128)}, u32[]{:S(2)}) copy-start(f32[512,256]{1,0:T(8,128)} %copy-done.1) | copy-start | bytes 1572868
  760.0 11.5 %collective-permute-start.40 = (f32[512,256]{1,0:T(8,128)S(1)}, f32[512,256]{1,0:T(8,128)S(1)}, u32[]{:S(2)}, u32[]{:S(2)}) collective-permute-start(f32[512,256]{1,0:T(8,128)S(1)} %multiply_add_fusion), channel_id=1, source_target_pairs={{0,2},{2,4},{4,6},{6,8},{8,10},{10,12},{12,14},{14,16},{16,18},{18... | collective-permute-start | bytes 1572872 | tf_op jit(solution)/shard_map/ppermute | solution.py:15
  760.1 11.4 %collective-permute-start.41 = (f32[512,256]{1,0:T(8,128)S(1)}, f32[512,256]{1,0:T(8,128)S(1)}, u32[]{:S(2)}, u32[]{:S(2)}) collective-permute-start(f32[512,256]{1,0:T(8,128)S(1)} %multiply_add_fusion), channel_id=1, source_target_pairs={{0,30},{2,0},{4,2},{6,4},{8,6},{10,8},{12,10},{14,12},{16,14},{18,... | collective-permute-start | bytes 1572872 | tf_op jit(solution)/shard_map/ppermute | solution.py:15
  771.6 35.4 %collective-permute-start.42 = (f32[3,512,256]{2,1,0:T(8,128)S(1)}, f32[3,512,256]{2,1,0:T(8,128)S(1)}, u32[]{:S(2)}, u32[]{:S(2)}) collective-permute-start(f32[3,512,256]{2,1,0:T(8,128)S(1)} %pad_maximum_fusion.2), channel_id=1, source_target_pairs={{0,1},{2,3},{4,5},{6,7},{8,9},{10,11},{12,13},{14,15},{16,17},{18,... | collective-permute-start | bytes 4718600 | tf_op jit(solution)/shard_map/ppermute | solution.py:21
  774.0 38.5 %collective-permute-start.43 = (f32[3,512,256]{2,1,0:T(8,128)S(1)}, f32[3,512,256]{2,1,0:T(8,128)S(1)}, u32[]{:S(2)}, u32[]{:S(2)}) collective-permute-start(f32[3,512,256]{2,1,0:T(8,128)S(1)} %pad_maximum_fusion.2), channel_id=1, source_target_pairs={{1,0},{3,2},{5,4},{7,6},{9,8},{11,10},{13,12},{15,14},{17,16},{19,... | collective-permute-start | bytes 4718600 | tf_op jit(solution)/shard_map/ppermute | solution.py:21
  (5 other events, 28.5 us)
